TPU v7x, 32 devices: a whole 2x2x4 slice. The times are simulated.
32 devices in a mesh: ctx: 16 (over z, x, core), tp: 2 (over y).
Axes of the slice: x: 2, y: 2, z: 4, core: 2. Of those that a mesh axis runs over, the one named last changes fastest.
Arguments:
- queries: bfloat16 [4096, 8192], P('ctx', 'tp'), may hold values from -6 to 6
- keys: bfloat16 [4096, 1024], P('ctx', 'tp'), may hold values from -6 to 6
- values: bfloat16 [4096, 1024], P('ctx', 'tp'), may hold values from -6 to 6
- documents: int32 [4096], replicated, may hold values from 0 to 3, never falling along the last dimension, each value on 1 to 2048 neighbouring positions
- hist_q: float32 [16, 64], P(None, 'tp'), may hold values from 0.75 to 5.4
- hist_kv: float32 [2, 16, 8], P(None, None, 'tp'), may hold values from 0.75 to 5.4
- out_weight: bfloat16 [8192, 8192], P(('tp', 'ctx')), may hold values from -0.0625 to 0.0625
Outputs:
- mixed: bfloat16 [4096, 8192], P('ctx', 'tp')
- new_hist_q: float32 [16, 64], P(None, 'tp')
- new_hist_kv: float32 [2, 16, 8], P(None, None, 'tp')
All inputs are finite; a program needn't handle non-finite values.
Results may differ from a plain program's by a relative error of at most 0.015.
Values may be sent and summed in bfloat16 or wider, within the bound.
A program may use at most 192 MiB of HBM per device.

v0:
```python
import math
import jax
import jax.numpy as jnp
from jax import lax
from jax.sharding import PartitionSpec as P


def on_device(queries, keys, values, documents, hist_q, hist_kv, out_weight):
    rows_here, width = queries.shape
    kv_heads = hist_kv.shape[2]
    heads_here = hist_q.shape[1]
    group = heads_here // kv_heads
    head_size = width // heads_here
    scale = 1.0 / math.sqrt(head_size)
    query_limit = jnp.max(hist_q, axis=0).reshape(kv_heads, group)
    pair_limit = jnp.max(hist_kv, axis=1)
    raw_query = queries.astype(jnp.float32).reshape(rows_here, kv_heads, group, head_size)
    clipped = jnp.clip(
        raw_query, -query_limit[None, :, :, None], query_limit[None, :, :, None]
    ).astype(jnp.bfloat16)
    query_peak = jnp.max(jnp.abs(raw_query.reshape(rows_here, heads_here, head_size)), axis=(0, 2))
    key_peak = jnp.max(
        jnp.abs(keys.astype(jnp.float32).reshape(rows_here, kv_heads, head_size)), axis=(0, 2)
    )
    value_peak = jnp.max(
        jnp.abs(values.astype(jnp.float32).reshape(rows_here, kv_heads, head_size)), axis=(0, 2)
    )
    current_query, current_pair = lax.pmax((query_peak, jnp.stack([key_peak, value_peak])), "ctx")
    query_start = lax.axis_index("ctx") * rows_here
    query_docs = lax.dynamic_slice_in_dim(documents, query_start, rows_here)
    query_pos = query_start + jnp.arange(rows_here, dtype=jnp.int32)

    def attend(state, key_block, value_block, key_start):
        top, total, acc = state
        count = key_block.shape[0]
        key_float = key_block.astype(jnp.float32).reshape(count, kv_heads, head_size)
        value_float = value_block.astype(jnp.float32).reshape(count, kv_heads, head_size)
        key_clip = jnp.clip(
            key_float, -pair_limit[0][None, :, None], pair_limit[0][None, :, None]
        ).astype(jnp.bfloat16)
        value_clip = jnp.clip(
            value_float, -pair_limit[1][None, :, None], pair_limit[1][None, :, None]
        ).astype(jnp.bfloat16)
        scores = (
            jnp.einsum("tgjd,bgd->gjtb", clipped, key_clip, preferred_element_type=jnp.float32)
            * scale
        )
        key_pos = key_start + jnp.arange(count, dtype=jnp.int32)
        key_docs = lax.dynamic_slice_in_dim(documents, key_start, count)
        allowed = (key_pos[None, :] <= query_pos[:, None]) & (
            key_docs[None, :] == query_docs[:, None]
        )
        new_top = jnp.maximum(top, jnp.max(jnp.where(allowed, scores, -1e30), axis=-1))
        weights = jnp.where(allowed, jnp.exp(scores - new_top[..., None]), 0.0)
        decay = jnp.exp(top - new_top)
        total = total * decay + jnp.sum(weights, axis=-1)
        acc = acc * decay[..., None] + jnp.einsum(
            "gjtb,bgd->gjtd",
            weights.astype(jnp.bfloat16),
            value_clip,
            preferred_element_type=jnp.float32,
        )
        return (new_top, total, acc)

    start_state = (
        jnp.full((kv_heads, group, rows_here), -1e30, jnp.float32),
        jnp.zeros((kv_heads, group, rows_here), jnp.float32),
        jnp.zeros((kv_heads, group, rows_here, head_size), jnp.float32),
    )
    key_piece = lax.all_gather(keys, "ctx", axis=0, tiled=True)
    value_piece = lax.all_gather(values, "ctx", axis=0, tiled=True)
    count = key_piece.shape[0]
    block = 512

    def inner(number, attn_state):
        key_block = lax.dynamic_slice_in_dim(key_piece, number * block, block)
        value_block = lax.dynamic_slice_in_dim(value_piece, number * block, block)
        key_start = number * block
        attn_state = attend(attn_state, key_block, value_block, key_start)
        return attn_state

    top, total, acc = lax.fori_loop(0, count // block, inner, start_state)
    attn = (
        jnp.transpose(acc / total[..., None], (2, 0, 1, 3))
        .reshape(rows_here, width)
        .astype(jnp.bfloat16)
    )
    new_hist_q = jnp.concatenate([current_query[None], hist_q[:-1]], axis=0)
    new_hist_kv = jnp.concatenate([current_pair[:, None], hist_kv[:, :-1]], axis=1)
    partial_rows = jnp.dot(
        attn,
        lax.all_gather(out_weight, "ctx", axis=0, tiled=True),
        preferred_element_type=jnp.float32,
    )
    mixed = lax.psum_scatter(
        partial_rows.astype(jnp.bfloat16), "tp", scatter_dimension=1, tiled=True
    )
    return (mixed, new_hist_q, new_hist_kv)


def solution(mesh):
    in_specs = (
        P("ctx", "tp"),
        P("ctx", "tp"),
        P("ctx", "tp"),
        P(),
        P(None, "tp"),
        P(None, None, "tp"),
        P(("tp", "ctx"), None),
    )
    out_specs = (P("ctx", "tp"), P(None, "tp"), P(None, None, "tp"))
    return jax.shard_map(
        on_device, mesh=mesh, in_specs=in_specs, out_specs=out_specs, check_vma=False
    )
```

profile of v0, /device:TPU:0, one launch (start us, length us, event | category | flops | bytes accessed | tf_op | source)
XLA Modules:
  0.0 530.1 jit_solution(18043814594572523001)
XLA Ops:
  19.6 43.7 %all-gather.4.cloned.1.call-done = bf16[4096,512]{1,0:T(8,128)(2,1)} async-done(((bf16[256,512]{1,0:T(8,128)(2,1)}), bf16[4096,512]{1,0:T(8,128)(2,1)}) %all-gather.4.cloned.1.call-update) | async-done | bytes 4194320 | tf_op jit(solution)/shard_map/all_gather | solution.py:70
  63.3 51.1 %all-gather.6.cloned.1.call-done = bf16[4096,512]{1,0:T(8,128)(2,1)} async-done(((bf16[256,512]{1,0:T(8,128)(2,1)}), bf16[4096,512]{1,0:T(8,128)(2,1)}) %all-gather.6.cloned.1.call-update) | async-done | bytes 4194320 | tf_op jit(solution)/shard_map/all_gather | solution.py:71
  114.4 244.9 %while.19 = (s32[]{:T(128)}, f32[4,8,256]{2,1,0:T(8,128)S(1)}, f32[4,8,256]{2,1,0:T(8,128)S(1)}, f32[4,8,256,128]{3,2,1,0:T(8,128)}, s32[4096]{0:T(1024)}, /*ind...) while((s32[]{:T(128)}, f32[4,8,256]{2,1,0:T(8,128)S(1)}, ...), condition=%wide.region_5.6_spmd.clone, body=%wide.region_2.5_spmd.clone.sunk | while | flops 2199298816 | bytes 65025316 | solution.py:82
  116.7 9.5 %fusion.42 = (f32[4,8,256]{2,1,0:T(8,128)S(1)}, f32[4,512,256,8]{2,1,3,0:T(8,128)}) fusion(pred[256,512]{0,1:T(8,128)(4,1)S(1)} %compare_and_fusion.2, bf16[256,4,8,128]{3,0,2,1:T(8,128)(2,1)S(1)} %get-tuple-element.489, bf16[64,4,8,128]{3,2,1,0:T(8,128)(2,1)S(1)} %get-tuple-element.438, bf16[4]{0:T(256)(128)(2,1)S(1)} %bitcast.109, ...), kind=kOutput, calls=%fused_computation.3.clone.1 | convolution fusion | flops 1087889408 | bytes 19562512 | tf_op jit(solution)/shard_map/while/body/eval_jaxpr/tgjd,bgd->gjtb/dot_general | solution.py:45
  126.2 9.2 %fusion.43 = f32[4,8,256]{2,1,0:T(8,128)S(1)} fusion(f32[4,512,256,8]{2,1,3,0:T(8,128)} %get-tuple-element.441, f32[4,8,256]{2,1,0:T(8,128)S(1)} %select_maximum_fusion.2, pred[256,512]{0,1:T(8,128)(4,1)S(1)} %compare_and_fusion.2), kind=kLoop, calls=%fused_computation.7.clone.1 | loop fusion | flops 16769024 | bytes 16973824 | tf_op jit(solution)/shard_map/while/body/eval_jaxpr/reduce_sum | solution.py:56
  135.4 10.3 %fusion.45 = f32[4,8,256,128]{3,2,1,0:T(8,128)} fusion(f32[4,8,256,128]{3,2,1,0:T(8,128)} %get-tuple-element.466, f32[4,8,256]{2,1,0:T(8,128)S(1)} %get-tuple-element.443, pred[]{:T(512)S(6)} %compare.3, f32[4,512,256,8]{2,1,3,0:T(8,128)} %get-tuple-element.441, f32[4,8,256]{2,1,0:T(8,128)S(1)} %select_maximum_fusion.2, ...), kind=kOutput, calls=%fused_computation.11.clone.1 | convolution fusion | flops 1094189056 | bytes 25886736 | tf_op jit(solution)/shard_map/while/body/eval_jaxpr/gjtb,bgd->gjtd/dot_general | solution.py:57
  155.5 9.7 %fusion.43 = f32[4,8,256]{2,1,0:T(8,128)S(1)} fusion(f32[4,512,256,8]{2,1,3,0:T(8,128)} %get-tuple-element.441, f32[4,8,256]{2,1,0:T(8,128)S(1)} %select_maximum_fusion.2, pred[256,512]{0,1:T(8,128)(4,1)S(1)} %compare_and_fusion.2), kind=kLoop, calls=%fused_computation.7.clone.1 | loop fusion | flops 16769024 | bytes 16973824 | tf_op jit(solution)/shard_map/while/body/eval_jaxpr/reduce_sum | solution.py:56
  165.2 11.4 %fusion.45 = f32[4,8,256,128]{3,2,1,0:T(8,128)} fusion(f32[4,8,256,128]{3,2,1,0:T(8,128)} %get-tuple-element.466, f32[4,8,256]{2,1,0:T(8,128)S(1)} %get-tuple-element.443, pred[]{:T(512)S(6)} %compare.3, f32[4,512,256,8]{2,1,3,0:T(8,128)} %get-tuple-element.441, f32[4,8,256]{2,1,0:T(8,128)S(1)} %select_maximum_fusion.2, ...), kind=kOutput, calls=%fused_computation.11.clone.1 | convolution fusion | flops 1094189056 | bytes 25886736 | tf_op jit(solution)/shard_map/while/body/eval_jaxpr/gjtb,bgd->gjtd/dot_general | solution.py:57
  186.4 9.2 %fusion.43 = f32[4,8,256]{2,1,0:T(8,128)S(1)} fusion(f32[4,512,256,8]{2,1,3,0:T(8,128)} %get-tuple-element.441, f32[4,8,256]{2,1,0:T(8,128)S(1)} %select_maximum_fusion.2, pred[256,512]{0,1:T(8,128)(4,1)S(1)} %compare_and_fusion.2), kind=kLoop, calls=%fused_computation.7.clone.1 | loop fusion | flops 16769024 | bytes 16973824 | tf_op jit(solution)/shard_map/while/body/eval_jaxpr/reduce_sum | solution.py:56
  195.6 11.0 %fusion.45 = f32[4,8,256,128]{3,2,1,0:T(8,128)} fusion(f32[4,8,256,128]{3,2,1,0:T(8,128)} %get-tuple-element.466, f32[4,8,256]{2,1,0:T(8,128)S(1)} %get-tuple-element.443, pred[]{:T(512)S(6)} %compare.3, f32[4,512,256,8]{2,1,3,0:T(8,128)} %get-tuple-element.441, f32[4,8,256]{2,1,0:T(8,128)S(1)} %select_maximum_fusion.2, ...), kind=kOutput, calls=%fused_computation.11.clone.1 | convolution fusion | flops 1094189056 | bytes 25886736 | tf_op jit(solution)/shard_map/while/body/eval_jaxpr/gjtb,bgd->gjtd/dot_general | solution.py:57
  216.4 9.4 %fusion.43 = f32[4,8,256]{2,1,0:T(8,128)S(1)} fusion(f32[4,512,256,8]{2,1,3,0:T(8,128)} %get-tuple-element.441, f32[4,8,256]{2,1,0:T(8,128)S(1)} %select_maximum_fusion.2, pred[256,512]{0,1:T(8,128)(4,1)S(1)} %compare_and_fusion.2), kind=kLoop, calls=%fused_computation.7.clone.1 | loop fusion | flops 16769024 | bytes 16973824 | tf_op jit(solution)/shard_map/while/body/eval_jaxpr/reduce_sum | solution.py:56
  225.8 11.2 %fusion.45 = f32[4,8,256,128]{3,2,1,0:T(8,128)} fusion(f32[4,8,256,128]{3,2,1,0:T(8,128)} %get-tuple-element.466, f32[4,8,256]{2,1,0:T(8,128)S(1)} %get-tuple-element.443, pred[]{:T(512)S(6)} %compare.3, f32[4,512,256,8]{2,1,3,0:T(8,128)} %get-tuple-element.441, f32[4,8,256]{2,1,0:T(8,128)S(1)} %select_maximum_fusion.2, ...), kind=kOutput, calls=%fused_computation.11.clone.1 | convolution fusion | flops 1094189056 | bytes 25886736 | tf_op jit(solution)/shard_map/while/body/eval_jaxpr/gjtb,bgd->gjtd/dot_general | solution.py:57
  246.5 9.8 %fusion.43 = f32[4,8,256]{2,1,0:T(8,128)S(1)} fusion(f32[4,512,256,8]{2,1,3,0:T(8,128)} %get-tuple-element.441, f32[4,8,256]{2,1,0:T(8,128)S(1)} %select_maximum_fusion.2, pred[256,512]{0,1:T(8,128)(4,1)S(1)} %compare_and_fusion.2), kind=kLoop, calls=%fused_computation.7.clone.1 | loop fusion | flops 16769024 | bytes 16973824 | tf_op jit(solution)/shard_map/while/body/eval_jaxpr/reduce_sum | solution.py:56
  256.3 11.5 %fusion.45 = f32[4,8,256,128]{3,2,1,0:T(8,128)} fusion(f32[4,8,256,128]{3,2,1,0:T(8,128)} %get-tuple-element.466, f32[4,8,256]{2,1,0:T(8,128)S(1)} %get-tuple-element.443, pred[]{:T(512)S(6)} %compare.3, f32[4,512,256,8]{2,1,3,0:T(8,128)} %get-tuple-element.441, f32[4,8,256]{2,1,0:T(8,128)S(1)} %select_maximum_fusion.2, ...), kind=kOutput, calls=%fused_computation.11.clone.1 | convolution fusion | flops 1094189056 | bytes 25886736 | tf_op jit(solution)/shard_map/while/body/eval_jaxpr/gjtb,bgd->gjtd/dot_general | solution.py:57
  277.5 9.6 %fusion.43 = f32[4,8,256]{2,1,0:T(8,128)S(1)} fusion(f32[4,512,256,8]{2,1,3,0:T(8,128)} %get-tuple-element.441, f32[4,8,256]{2,1,0:T(8,128)S(1)} %select_maximum_fusion.2, pred[256,512]{0,1:T(8,128)(4,1)S(1)} %compare_and_fusion.2), kind=kLoop, calls=%fused_computation.7.clone.1 | loop fusion | flops 16769024 | bytes 16973824 | tf_op jit(solution)/shard_map/while/body/eval_jaxpr/reduce_sum | solution.py:56
  287.1 11.3 %fusion.45 = f32[4,8,256,128]{3,2,1,0:T(8,128)} fusion(f32[4,8,256,128]{3,2,1,0:T(8,128)} %get-tuple-element.466, f32[4,8,256]{2,1,0:T(8,128)S(1)} %get-tuple-element.443, pred[]{:T(512)S(6)} %compare.3, f32[4,512,256,8]{2,1,3,0:T(8,128)} %get-tuple-element.441, f32[4,8,256]{2,1,0:T(8,128)S(1)} %select_maximum_fusion.2, ...), kind=kOutput, calls=%fused_computation.11.clone.1 | convolution fusion | flops 1094189056 | bytes 25886736 | tf_op jit(solution)/shard_map/while/body/eval_jaxpr/gjtb,bgd->gjtd/dot_general | solution.py:57
  308.2 9.2 %fusion.43 = f32[4,8,256]{2,1,0:T(8,128)S(1)} fusion(f32[4,512,256,8]{2,1,3,0:T(8,128)} %get-tuple-element.441, f32[4,8,256]{2,1,0:T(8,128)S(1)} %select_maximum_fusion.2, pred[256,512]{0,1:T(8,128)(4,1)S(1)} %compare_and_fusion.2), kind=kLoop, calls=%fused_computation.7.clone.1 | loop fusion | flops 16769024 | bytes 16973824 | tf_op jit(solution)/shard_map/while/body/eval_jaxpr/reduce_sum | solution.py:56
  317.5 11.1 %fusion.45 = f32[4,8,256,128]{3,2,1,0:T(8,128)} fusion(f32[4,8,256,128]{3,2,1,0:T(8,128)} %get-tuple-element.466, f32[4,8,256]{2,1,0:T(8,128)S(1)} %get-tuple-element.443, pred[]{:T(512)S(6)} %compare.3, f32[4,512,256,8]{2,1,3,0:T(8,128)} %get-tuple-element.441, f32[4,8,256]{2,1,0:T(8,128)S(1)} %select_maximum_fusion.2, ...), kind=kOutput, calls=%fused_computation.11.clone.1 | convolution fusion | flops 1094189056 | bytes 25886736 | tf_op jit(solution)/shard_map/while/body/eval_jaxpr/gjtb,bgd->gjtd/dot_general | solution.py:57
  338.2 9.5 %fusion.43 = f32[4,8,256]{2,1,0:T(8,128)S(1)} fusion(f32[4,512,256,8]{2,1,3,0:T(8,128)} %get-tuple-element.441, f32[4,8,256]{2,1,0:T(8,128)S(1)} %select_maximum_fusion.2, pred[256,512]{0,1:T(8,128)(4,1)S(1)} %compare_and_fusion.2), kind=kLoop, calls=%fused_computation.7.clone.1 | loop fusion | flops 16769024 | bytes 16973824 | tf_op jit(solution)/shard_map/while/body/eval_jaxpr/reduce_sum | solution.py:56
  347.7 11.6 %fusion.45 = f32[4,8,256,128]{3,2,1,0:T(8,128)} fusion(f32[4,8,256,128]{3,2,1,0:T(8,128)} %get-tuple-element.466, f32[4,8,256]{2,1,0:T(8,128)S(1)} %get-tuple-element.443, pred[]{:T(512)S(6)} %compare.3, f32[4,512,256,8]{2,1,3,0:T(8,128)} %get-tuple-element.441, f32[4,8,256]{2,1,0:T(8,128)S(1)} %select_maximum_fusion.2, ...), kind=kOutput, calls=%fused_computation.11.clone.1 | convolution fusion | flops 1094189056 | bytes 25886736 | tf_op jit(solution)/shard_map/while/body/eval_jaxpr/gjtb,bgd->gjtd/dot_general | solution.py:57
  367.4 73.3 %all-gather.8.cloned.1.call-done = bf16[4096,8192]{1,0:T(8,128)(2,1)} async-done(((bf16[256,8192]{1,0:T(8,128)(2,1)}), bf16[4096,8192]{1,0:T(8,128)(2,1)}) %all-gather.8.cloned.1.call-update) | async-done | bytes 67108880 | tf_op jit(solution)/shard_map/all_gather | solution.py:92
  440.7 28.3 %convolution_convert_fusion = bf16[256,8192]{1,0:T(8,128)(2,1)} fusion(bf16[256,4096]{0,1:T(8,128)(2,1)S(1)} %bitcast.108, bf16[4096,8192]{1,0:T(8,128)(2,1)} %all-gather.8.cloned.1.call-done), kind=kOutput, calls=%fused_computation.38 | convolution fusion | flops 17181966336 | bytes 73400320 | tf_op jit(solution)/shard_map/dot_general | solution.py:90
  471.5 32.6 %all-reduce = (f32[1,32]{1,0:T(1,128)S(1)}, f32[2,1,4]{2,0,1:T(2,128)S(1)}) all-reduce(f32[1,32]{1,0:T(1,128)S(1)} %bitcast.114, f32[2,1,4]{2,0,1:T(2,128)S(1)} %maximum_bitcast_fusion), channel_id=1, replica_groups=mesh['ctx'=16,'tp'=2] {'ctx'}, use_global_device_ids=true, to_apply=%region_9.10 | all-reduce | flops 40 | bytes 320 | tf_op jit(solution)/shard_map/pmax | solution.py:28
  505.5 18.1 %reduce-scatter.2.cloned.1.call-done = bf16[256,4096]{1,0:T(8,128)(2,1)} async-done(((bf16[256,8192]{1,0:T(8,128)(2,1)}), bf16[256,4096]{1,0:T(8,128)(2,1)}) %reduce-scatter.2.cloned.1.call-update) | async-done | bytes 2097168 | tf_op jit(solution)/shard_map/reduce_scatter | solution.py:95
  (126 shorter events, 94.5 us)
Async XLA Ops:
  7.2 56.2 %all-gather.4.cloned.1.call-start = ((), (), s32[]{:S(2)}) async-start(), calls=%async_computation.1 | async-start | bytes 4456448 | tf_op jit(solution)/shard_map/all_gather | solution.py:70
  7.9 106.5 %all-gather.6.cloned.1.call-start = ((), (), s32[]{:S(2)}) async-start(), calls=%async_computation.2 | async-start | bytes 4456448 | tf_op jit(solution)/shard_map/all_gather | solution.py:71
  8.6 4.1 copy-start.4
  8.7 432.0 %all-gather.8.cloned.1.call-start = ((), (), s32[]{:S(2)}) async-start(), calls=%async_computation.3 | async-start | bytes 71303168 | tf_op jit(solution)/shard_map/all_gather | solution.py:92
  9.4 514.2 %reduce-scatter.2.cloned.1.call-start = ((), (), s32[]{:S(2)}) async-start(), calls=%async_computation.4 | async-start | bytes 6291456 | tf_op jit(solution)/shard_map/reduce_scatter | solution.py:95
  12.8 1.4 copy-start
  14.2 4.6 copy-start.6
  469.0 0.9 copy-start.2
  469.0 1.1 copy-start.3
  469.0 1.8 copy-start.1
  469.0 35.9 %copy-start.5 = (f32[16,32]{1,0:T(8,128)S(1)}, f32[16,32]{1,0:T(8,128)}, u32[]{:S(2)}) copy-start(f32[16,32]{1,0:T(8,128)} %param.13) | copy-start | bytes 6148
Sparse Core Ops, SparseCore 0:
  10.1 53.1 all-gather.3
  65.5 48.8 all-gather.5
  116.0 324.6 all-gather.7
  469.2 54.3 reduce-scatter.1
where the time goes:
time: 531 us; the launch traced here: 530 us
  waiting for transfers between devices  188 us (35%)
  matrix products  179 us (34%)
  other arithmetic  84.3 us (16%)
  blocking collectives  32.6 us (6%)
  local copies, waits for them, and re-layouts  31.9 us (6%)
  between operations  13.9 us (3%)
    dot_general x8, matrix products, attend(): jnp.einsum('gjtb,bgd->gjtd', weights.astype(jnp.bfloat16), value_clip, pr...  89.3 us
    reduce_sum x8, other arithmetic, attend(): total = total * decay + jnp.sum(weights, axis=-1)  75.6 us
    all_gather x1, waiting for transfers between devices, on_device(): lax.all_gather(out_weight, 'ctx', axis=0, tiled=True)  73.3 us
    dot_general x8, matrix products, attend(): jnp.einsum('tgjd,bgd->gjtb', clipped, key_clip, preferred_element_type=jn...  61.2 us
    all_gather x1, waiting for transfers between devices, on_device(): value_piece = lax.all_gather(values, 'ctx', axis=0, tiled=True)  51.1 us
    all_gather x1, waiting for transfers between devices, on_device(): key_piece = lax.all_gather(keys, 'ctx', axis=0, tiled=True)  43.7 us
    pmax x1, blocking collectives, on_device(): lax.pmax((query_peak, jnp.stack([key_peak, value_peak])), 'ctx')  32.6 us
    dot_general x1, matrix products, on_device(): jnp.dot(attn, lax.all_gather(out_weight, 'ctx', axis=0, tiled=True), pref...  28.3 us
  transfers between devices with their start and end apart: 4, of which 4 were waited for; matrix products, arithmetic and copies ran while one was open for 50% of the time, Pallas kernels for 0%

commit v1 on v0

--- a/solution.py
+++ b/solution.py
@@ -67,8 +67,11 @@
         jnp.zeros((kv_heads, group, rows_here), jnp.float32),
         jnp.zeros((kv_heads, group, rows_here, head_size), jnp.float32),
     )
-    key_piece = lax.all_gather(keys, "ctx", axis=0, tiled=True)
-    value_piece = lax.all_gather(values, "ctx", axis=0, tiled=True)
+    key_piece, value_piece = jnp.split(
+        lax.all_gather(jnp.concatenate([keys, values], axis=1), "ctx", axis=0, tiled=True),
+        [keys.shape[1]],
+        axis=1,
+    )
     count = key_piece.shape[0]
     block = 512
 

time: 531 us -> 504 us (0.949)
  waiting for transfers between devices: 188 us -> 156 us
  local copies, waits for them, and re-layouts: 31.9 us -> 37.8 us
    all_gather x2 -> x1, waiting for transfers between devices: 94.8 us -> 67 us  [on_device(): lax.all_gather(jnp.concatenate([keys, values], axis=1), 'ctx', axis=0, ti...]
    split x0 -> x1, local copies, waits for them, and re-layouts: none -> 5.69 us  [on_device(): jnp.split(lax.all_gather(jnp.concatenate([keys, values], axis=1), 'ctx',...]
  transfers between devices with their start and end apart: 4 -> 3, of which waited for: 4 -> 3; matrix products, arithmetic and copies ran while one was open for 50% -> 53% of each run, Pallas kernels for 0% -> 0%
where the time goes in v1:
time: 504 us; the launch traced here: 503 us
  matrix products  176 us (35%)
  waiting for transfers between devices  156 us (31%)
  other arithmetic  86.4 us (17%)
  local copies, waits for them, and re-layouts  37.8 us (7%)
  blocking collectives  32.6 us (6%)
  between operations  13.9 us (3%)
    dot_general x8, matrix products, attend(): jnp.einsum('gjtb,bgd->gjtd', weights.astype(jnp.bfloat16), value_clip, pr...  89 us
    reduce_sum x8, other arithmetic, attend(): total = total * decay + jnp.sum(weights, axis=-1)  75.9 us
    all_gather x1, waiting for transfers between devices, on_device(): lax.all_gather(out_weight, 'ctx', axis=0, tiled=True)  69.7 us
    all_gather x1, waiting for transfers between devices, on_device(): lax.all_gather(jnp.concatenate([keys, values], axis=1), 'ctx', axis=0, ti...  67 us
    dot_general x8, matrix products, attend(): jnp.einsum('tgjd,bgd->gjtb', clipped, key_clip, preferred_element_type=jn...  59.1 us
    pmax x1, blocking collectives, on_device(): lax.pmax((query_peak, jnp.stack([key_peak, value_peak])), 'ctx')  32.6 us
    dot_general x1, matrix products, on_device(): jnp.dot(attn, lax.all_gather(out_weight, 'ctx', axis=0, tiled=True), pref...  28.3 us
    reduce_scatter x1, waiting for transfers between devices, on_device(): lax.psum_scatter(partial_rows.astype(jnp.bfloat16), 'tp', scatter_dimensi...  18.1 us
  transfers between devices with their start and end apart: 3, of which 3 were waited for; matrix products, arithmetic and copies ran while one was open for 53% of the time, Pallas kernels for 0%

profile of v1, /device:TPU:0, one launch (start us, length us, event | category | flops | bytes accessed | tf_op | source)
XLA Modules:
  0.0 502.9 jit_solution(13579531483977178367)
XLA Ops:
  20.2 67.0 %all-gather.3.cloned.1.call-done = bf16[4096,1024]{1,0:T(8,128)(2,1)} async-done(((bf16[256,1024]{1,0:T(8,128)(2,1)}), bf16[4096,1024]{1,0:T(8,128)(2,1)}) %all-gather.3.cloned.1.call-update) | async-done | bytes 8388624 | tf_op jit(solution)/shard_map/all_gather | solution.py:71
  92.9 242.9 %while.19 = (s32[]{:T(128)}, f32[4,8,256]{2,1,0:T(8,128)S(1)}, f32[4,8,256]{2,1,0:T(8,128)S(1)}, f32[4,8,256,128]{3,2,1,0:T(8,128)}, s32[4096]{0:T(1024)}, /*ind...) while((s32[]{:T(128)}, f32[4,8,256]{2,1,0:T(8,128)S(1)}, ...), condition=%wide.region_5.6_spmd.clone, body=%wide.region_2.5_spmd.clone.sunk | while | flops 2199298816 | bytes 65025316 | solution.py:85
  102.8 9.2 %fusion.44 = f32[4,8,256]{2,1,0:T(8,128)S(1)} fusion(f32[4,512,256,8]{2,1,3,0:T(8,128)} %get-tuple-element.443, f32[4,8,256]{2,1,0:T(8,128)S(1)} %select_maximum_fusion.2, pred[256,512]{0,1:T(8,128)(4,1)S(1)} %compare_and_fusion.2), kind=kLoop, calls=%fused_computation.7.clone.1 | loop fusion | flops 16769024 | bytes 16973824 | tf_op jit(solution)/shard_map/while/body/eval_jaxpr/reduce_sum | solution.py:56
  112.0 10.0 %fusion.46 = f32[4,8,256,128]{3,2,1,0:T(8,128)} fusion(f32[4,8,256,128]{3,2,1,0:T(8,128)} %get-tuple-element.468, f32[4,8,256]{2,1,0:T(8,128)S(1)} %get-tuple-element.445, pred[]{:T(512)S(6)} %compare.3, f32[4,512,256,8]{2,1,3,0:T(8,128)} %get-tuple-element.443, f32[4,8,256]{2,1,0:T(8,128)S(1)} %select_maximum_fusion.2, ...), kind=kOutput, calls=%fused_computation.11.clone.1 | convolution fusion | flops 1094189056 | bytes 25886736 | tf_op jit(solution)/shard_map/while/body/eval_jaxpr/gjtb,bgd->gjtd/dot_general | solution.py:57
  131.8 9.4 %fusion.44 = f32[4,8,256]{2,1,0:T(8,128)S(1)} fusion(f32[4,512,256,8]{2,1,3,0:T(8,128)} %get-tuple-element.443, f32[4,8,256]{2,1,0:T(8,128)S(1)} %select_maximum_fusion.2, pred[256,512]{0,1:T(8,128)(4,1)S(1)} %compare_and_fusion.2), kind=kLoop, calls=%fused_computation.7.clone.1 | loop fusion | flops 16769024 | bytes 16973824 | tf_op jit(solution)/shard_map/while/body/eval_jaxpr/reduce_sum | solution.py:56
  141.2 11.6 %fusion.46 = f32[4,8,256,128]{3,2,1,0:T(8,128)} fusion(f32[4,8,256,128]{3,2,1,0:T(8,128)} %get-tuple-element.468, f32[4,8,256]{2,1,0:T(8,128)S(1)} %get-tuple-element.445, pred[]{:T(512)S(6)} %compare.3, f32[4,512,256,8]{2,1,3,0:T(8,128)} %get-tuple-element.443, f32[4,8,256]{2,1,0:T(8,128)S(1)} %select_maximum_fusion.2, ...), kind=kOutput, calls=%fused_computation.11.clone.1 | convolution fusion | flops 1094189056 | bytes 25886736 | tf_op jit(solution)/shard_map/while/body/eval_jaxpr/gjtb,bgd->gjtd/dot_general | solution.py:57
  162.4 9.8 %fusion.44 = f32[4,8,256]{2,1,0:T(8,128)S(1)} fusion(f32[4,512,256,8]{2,1,3,0:T(8,128)} %get-tuple-element.443, f32[4,8,256]{2,1,0:T(8,128)S(1)} %select_maximum_fusion.2, pred[256,512]{0,1:T(8,128)(4,1)S(1)} %compare_and_fusion.2), kind=kLoop, calls=%fused_computation.7.clone.1 | loop fusion | flops 16769024 | bytes 16973824 | tf_op jit(solution)/shard_map/while/body/eval_jaxpr/reduce_sum | solution.py:56
  172.2 11.4 %fusion.46 = f32[4,8,256,128]{3,2,1,0:T(8,128)} fusion(f32[4,8,256,128]{3,2,1,0:T(8,128)} %get-tuple-element.468, f32[4,8,256]{2,1,0:T(8,128)S(1)} %get-tuple-element.445, pred[]{:T(512)S(6)} %compare.3, f32[4,512,256,8]{2,1,3,0:T(8,128)} %get-tuple-element.443, f32[4,8,256]{2,1,0:T(8,128)S(1)} %select_maximum_fusion.2, ...), kind=kOutput, calls=%fused_computation.11.clone.1 | convolution fusion | flops 1094189056 | bytes 25886736 | tf_op jit(solution)/shard_map/while/body/eval_jaxpr/gjtb,bgd->gjtd/dot_general | solution.py:57
  193.4 9.5 %fusion.44 = f32[4,8,256]{2,1,0:T(8,128)S(1)} fusion(f32[4,512,256,8]{2,1,3,0:T(8,128)} %get-tuple-element.443, f32[4,8,256]{2,1,0:T(8,128)S(1)} %select_maximum_fusion.2, pred[256,512]{0,1:T(8,128)(4,1)S(1)} %compare_and_fusion.2), kind=kLoop, calls=%fused_computation.7.clone.1 | loop fusion | flops 16769024 | bytes 16973824 | tf_op jit(solution)/shard_map/while/body/eval_jaxpr/reduce_sum | solution.py:56
  202.9 10.9 %fusion.46 = f32[4,8,256,128]{3,2,1,0:T(8,128)} fusion(f32[4,8,256,128]{3,2,1,0:T(8,128)} %get-tuple-element.468, f32[4,8,256]{2,1,0:T(8,128)S(1)} %get-tuple-element.445, pred[]{:T(512)S(6)} %compare.3, f32[4,512,256,8]{2,1,3,0:T(8,128)} %get-tuple-element.443, f32[4,8,256]{2,1,0:T(8,128)S(1)} %select_maximum_fusion.2, ...), kind=kOutput, calls=%fused_computation.11.clone.1 | convolution fusion | flops 1094189056 | bytes 25886736 | tf_op jit(solution)/shard_map/while/body/eval_jaxpr/gjtb,bgd->gjtd/dot_general | solution.py:57
  216.1 7.5 %fusion.43 = (f32[4,8,256]{2,1,0:T(8,128)S(1)}, f32[4,512,256,8]{2,1,3,0:T(8,128)}) fusion(pred[256,512]{0,1:T(8,128)(4,1)S(1)} %compare_and_fusion.2, bf16[256,4,8,128]{3,0,2,1:T(8,128)(2,1)S(1)} %get-tuple-element.491, bf16[64,4,8,128]{3,2,1,0:T(8,128)(2,1)S(1)} %get-tuple-element.440, bf16[4]{0:T(256)(128)(2,1)S(1)} %bitcast.109, ...), kind=kOutput, calls=%fused_computation.3.clone.1 | convolution fusion | flops 1087889408 | bytes 19562512 | tf_op jit(solution)/shard_map/while/body/eval_jaxpr/tgjd,bgd->gjtb/dot_general | solution.py:45
  223.6 9.3 %fusion.44 = f32[4,8,256]{2,1,0:T(8,128)S(1)} fusion(f32[4,512,256,8]{2,1,3,0:T(8,128)} %get-tuple-element.443, f32[4,8,256]{2,1,0:T(8,128)S(1)} %select_maximum_fusion.2, pred[256,512]{0,1:T(8,128)(4,1)S(1)} %compare_and_fusion.2), kind=kLoop, calls=%fused_computation.7.clone.1 | loop fusion | flops 16769024 | bytes 16973824 | tf_op jit(solution)/shard_map/while/body/eval_jaxpr/reduce_sum | solution.py:56
  232.9 11.1 %fusion.46 = f32[4,8,256,128]{3,2,1,0:T(8,128)} fusion(f32[4,8,256,128]{3,2,1,0:T(8,128)} %get-tuple-element.468, f32[4,8,256]{2,1,0:T(8,128)S(1)} %get-tuple-element.445, pred[]{:T(512)S(6)} %compare.3, f32[4,512,256,8]{2,1,3,0:T(8,128)} %get-tuple-element.443, f32[4,8,256]{2,1,0:T(8,128)S(1)} %select_maximum_fusion.2, ...), kind=kOutput, calls=%fused_computation.11.clone.1 | convolution fusion | flops 1094189056 | bytes 25886736 | tf_op jit(solution)/shard_map/while/body/eval_jaxpr/gjtb,bgd->gjtd/dot_general | solution.py:57
  253.6 9.8 %fusion.44 = f32[4,8,256]{2,1,0:T(8,128)S(1)} fusion(f32[4,512,256,8]{2,1,3,0:T(8,128)} %get-tuple-element.443, f32[4,8,256]{2,1,0:T(8,128)S(1)} %select_maximum_fusion.2, pred[256,512]{0,1:T(8,128)(4,1)S(1)} %compare_and_fusion.2), kind=kLoop, calls=%fused_computation.7.clone.1 | loop fusion | flops 16769024 | bytes 16973824 | tf_op jit(solution)/shard_map/while/body/eval_jaxpr/reduce_sum | solution.py:56
  263.5 11.5 %fusion.46 = f32[4,8,256,128]{3,2,1,0:T(8,128)} fusion(f32[4,8,256,128]{3,2,1,0:T(8,128)} %get-tuple-element.468, f32[4,8,256]{2,1,0:T(8,128)S(1)} %get-tuple-element.445, pred[]{:T(512)S(6)} %compare.3, f32[4,512,256,8]{2,1,3,0:T(8,128)} %get-tuple-element.443, f32[4,8,256]{2,1,0:T(8,128)S(1)} %select_maximum_fusion.2, ...), kind=kOutput, calls=%fused_computation.11.clone.1 | convolution fusion | flops 1094189056 | bytes 25886736 | tf_op jit(solution)/shard_map/while/body/eval_jaxpr/gjtb,bgd->gjtd/dot_general | solution.py:57
  284.7 9.7 %fusion.44 = f32[4,8,256]{2,1,0:T(8,128)S(1)} fusion(f32[4,512,256,8]{2,1,3,0:T(8,128)} %get-tuple-element.443, f32[4,8,256]{2,1,0:T(8,128)S(1)} %select_maximum_fusion.2, pred[256,512]{0,1:T(8,128)(4,1)S(1)} %compare_and_fusion.2), kind=kLoop, calls=%fused_computation.7.clone.1 | loop fusion | flops 16769024 | bytes 16973824 | tf_op jit(solution)/shard_map/while/body/eval_jaxpr/reduce_sum | solution.py:56
  294.4 11.4 %fusion.46 = f32[4,8,256,128]{3,2,1,0:T(8,128)} fusion(f32[4,8,256,128]{3,2,1,0:T(8,128)} %get-tuple-element.468, f32[4,8,256]{2,1,0:T(8,128)S(1)} %get-tuple-element.445, pred[]{:T(512)S(6)} %compare.3, f32[4,512,256,8]{2,1,3,0:T(8,128)} %get-tuple-element.443, f32[4,8,256]{2,1,0:T(8,128)S(1)} %select_maximum_fusion.2, ...), kind=kOutput, calls=%fused_computation.11.clone.1 | convolution fusion | flops 1094189056 | bytes 25886736 | tf_op jit(solution)/shard_map/while/body/eval_jaxpr/gjtb,bgd->gjtd/dot_general | solution.py:57
  308.0 7.5 %fusion.43 = (f32[4,8,256]{2,1,0:T(8,128)S(1)}, f32[4,512,256,8]{2,1,3,0:T(8,128)}) fusion(pred[256,512]{0,1:T(8,128)(4,1)S(1)} %compare_and_fusion.2, bf16[256,4,8,128]{3,0,2,1:T(8,128)(2,1)S(1)} %get-tuple-element.491, bf16[64,4,8,128]{3,2,1,0:T(8,128)(2,1)S(1)} %get-tuple-element.440, bf16[4]{0:T(256)(128)(2,1)S(1)} %bitcast.109, ...), kind=kOutput, calls=%fused_computation.3.clone.1 | convolution fusion | flops 1087889408 | bytes 19562512 | tf_op jit(solution)/shard_map/while/body/eval_jaxpr/tgjd,bgd->gjtb/dot_general | solution.py:45
  315.5 9.2 %fusion.44 = f32[4,8,256]{2,1,0:T(8,128)S(1)} fusion(f32[4,512,256,8]{2,1,3,0:T(8,128)} %get-tuple-element.443, f32[4,8,256]{2,1,0:T(8,128)S(1)} %select_maximum_fusion.2, pred[256,512]{0,1:T(8,128)(4,1)S(1)} %compare_and_fusion.2), kind=kLoop, calls=%fused_computation.7.clone.1 | loop fusion | flops 16769024 | bytes 16973824 | tf_op jit(solution)/shard_map/while/body/eval_jaxpr/reduce_sum | solution.py:56
  324.7 11.0 %fusion.46 = f32[4,8,256,128]{3,2,1,0:T(8,128)} fusion(f32[4,8,256,128]{3,2,1,0:T(8,128)} %get-tuple-element.468, f32[4,8,256]{2,1,0:T(8,128)S(1)} %get-tuple-element.445, pred[]{:T(512)S(6)} %compare.3, f32[4,512,256,8]{2,1,3,0:T(8,128)} %get-tuple-element.443, f32[4,8,256]{2,1,0:T(8,128)S(1)} %select_maximum_fusion.2, ...), kind=kOutput, calls=%fused_computation.11.clone.1 | convolution fusion | flops 1094189056 | bytes 25886736 | tf_op jit(solution)/shard_map/while/body/eval_jaxpr/gjtb,bgd->gjtd/dot_general | solution.py:57
  343.8 69.7 %all-gather.5.cloned.1.call-done = bf16[4096,8192]{1,0:T(8,128)(2,1)} async-done(((bf16[256,8192]{1,0:T(8,128)(2,1)}), bf16[4096,8192]{1,0:T(8,128)(2,1)}) %all-gather.5.cloned.1.call-update) | async-done | bytes 67108880 | tf_op jit(solution)/shard_map/all_gather | solution.py:95
  413.5 28.3 %convolution_convert_fusion = bf16[256,8192]{1,0:T(8,128)(2,1)} fusion(bf16[256,4096]{0,1:T(8,128)(2,1)S(1)} %bitcast.108, bf16[4096,8192]{1,0:T(8,128)(2,1)} %all-gather.5.cloned.1.call-done), kind=kOutput, calls=%fused_computation.38 | convolution fusion | flops 17181966336 | bytes 73400320 | tf_op jit(solution)/shard_map/dot_general | solution.py:93
  444.4 32.6 %all-reduce = (f32[1,32]{1,0:T(1,128)S(1)}, f32[2,1,4]{2,0,1:T(2,128)S(1)}) all-reduce(f32[1,32]{1,0:T(1,128)S(1)} %bitcast.114, f32[2,1,4]{2,0,1:T(2,128)S(1)} %maximum_bitcast_fusion), channel_id=1, replica_groups=mesh['ctx'=16,'tp'=2] {'ctx'}, use_global_device_ids=true, to_apply=%region_9.10 | all-reduce | flops 40 | bytes 320 | tf_op jit(solution)/shard_map/pmax | solution.py:28
  478.3 18.1 %reduce-scatter.2.cloned.1.call-done = bf16[256,4096]{1,0:T(8,128)(2,1)} async-done(((bf16[256,8192]{1,0:T(8,128)(2,1)}), bf16[256,4096]{1,0:T(8,128)(2,1)}) %reduce-scatter.2.cloned.1.call-update) | async-done | bytes 2097168 | tf_op jit(solution)/shard_map/reduce_scatter | solution.py:98
  (127 shorter events, 93.3 us)
Async XLA Ops:
  7.2 80.0 %all-gather.3.cloned.1.call-start = ((), (), s32[]{:S(2)}) async-start(), calls=%async_computation.1 | async-start | bytes 8912896 | tf_op jit(solution)/shard_map/all_gather | solution.py:71
  9.1 4.1 copy-start.4
  9.2 404.4 %all-gather.5.cloned.1.call-start = ((), (), s32[]{:S(2)}) async-start(), calls=%async_computation.2 | async-start | bytes 71303168 | tf_op jit(solution)/shard_map/all_gather | solution.py:95
  9.9 486.5 %reduce-scatter.2.cloned.1.call-start = ((), (), s32[]{:S(2)}) async-start(), calls=%async_computation.3 | async-start | bytes 6291456 | tf_op jit(solution)/shard_map/reduce_scatter | solution.py:98
  13.3 1.4 copy-start
  14.7 4.6 copy-start.6
  441.9 0.9 copy-start.2
  441.9 1.1 copy-start.3
  441.9 1.8 copy-start.1
  441.9 35.2 %copy-start.7 = (f32[2,16,4]{1,2,0:T(4,128)S(1)}, f32[2,16,4]{1,2,0:T(4,128)}, u32[]{:S(2)}) copy-start(f32[2,16,4]{1,2,0:T(4,128)} %param.14) | copy-start | bytes 1540
  441.9 35.8 %copy-start.5 = (f32[16,32]{1,0:T(8,128)S(1)}, f32[16,32]{1,0:T(8,128)}, u32[]{:S(2)}) copy-start(f32[16,32]{1,0:T(8,128)} %param.13) | copy-start | bytes 6148
Sparse Core Ops, SparseCore 0:
  10.1 77.0 all-gather.2
  88.8 324.7 all-gather.4
  442.0 54.3 reduce-scatter.1
